TPU v7x, 32 devices: a whole 2x2x4 slice. The times are simulated.
32 devices in a mesh: ep: 4 (over y, x), edp: 4 (over z), tp: 2 (over core).
Axes of the slice: x: 2, y: 2, z: 4, core: 2. Of those that a mesh axis runs over, the one named last changes fastest.
Arguments:
- tokens: bfloat16 [2048, 4096], P(('ep', 'edp'), 'tp'), may hold values from -6 to 6
- cotangent: bfloat16 [2048, 4096], P(('ep', 'edp'), 'tp'), may hold values from -6 to 6
- expert_ids: int32 [2048, 8], P(('ep', 'edp')), may hold values from 0 to 127, all different within a row; in each aligned block of 128 rows (0 to 127, 128 to 255, ...) at most 10 rows name the same one
- route_weights: float32 [2048, 8], P(('ep', 'edp')), may hold values from 0.1 to 1
- expert_weights: bfloat16 [3, 1536, 4096], P(None, ('ep', 'tp')), may hold values from -0.15625 to 0.15625
Outputs:
- mixed: bfloat16 [2048, 4096], P(('ep', 'edp'), 'tp')
- grad_tokens: bfloat16 [2048, 4096], P(('ep', 'edp'), 'tp')
- weight_grads: float32 [3, 1536, 4096], P(None, ('ep', 'tp'), 'edp')
Inputs may be any that keep to these rules, and one draw needn't show every extreme that they name: `expert_ids`: each token names 8 different experts; within the tokens of one (ep, edp) index no expert is named by more than 10 tokens.
All inputs are finite; a program needn't handle non-finite values.
Results may differ from a plain program's by a relative error of at most 0.017.
Values may be sent and summed in bfloat16 or wider, within the bound.
A program may use at most 64 MiB of HBM per device.

v0:
```python
import jax
import jax.numpy as jnp
from jax import lax
from jax.sharding import PartitionSpec as P

CAP = 10


def route_tables(expert_ids, route_weights, window):
    tok_rows, top_count = expert_ids.shape
    flat_ids = expert_ids.reshape(-1)
    matches = (flat_ids[:, None] == jnp.arange(window, dtype=jnp.int32)[None, :]).astype(jnp.int32)
    slot_index = jnp.sum(matches * (jnp.cumsum(matches, axis=0) - 1), axis=1)
    in_slot = (slot_index[:, None] == jnp.arange(CAP, dtype=jnp.int32)[None, :]).astype(jnp.float32)
    placed = matches.astype(jnp.float32)[:, :, None] * in_slot[:, None, :]
    placed = placed.reshape(tok_rows, top_count, window, CAP)
    select = jnp.sum(placed, axis=1)
    weighted = jnp.sum(placed * route_weights[:, :, None, None], axis=1)
    return (select, weighted)


def pack_rows(select, weighted, features, grads_in):
    packed = jnp.einsum(
        "tec,td->ecd", select.astype(jnp.bfloat16), features, preferred_element_type=jnp.float32
    ).astype(jnp.bfloat16)
    scaled = jnp.einsum(
        "tec,td->ecd", weighted, grads_in.astype(jnp.float32), precision=lax.Precision.HIGHEST
    ).astype(jnp.bfloat16)
    return (jnp.repeat(packed, 4, axis=0), jnp.repeat(scaled, 4, axis=0))


def replica_sum(left, right):
    partial_sums = jnp.einsum("prs,prd->psd", left, right, preferred_element_type=jnp.float32)
    rounded = lax.optimization_barrier(partial_sums.astype(jnp.bfloat16)).astype(jnp.float32)
    return jnp.sum(rounded, axis=0)


def shards(tokens, cotangent, expert_ids, route_weights, expert_weights):
    n_devices = lax.axis_size("ep")
    window = n_devices // 4
    select, weighted = route_tables(expert_ids, route_weights, window)
    whole_tokens, whole_grads = (
        lax.all_gather(tokens, "tp", axis=1, tiled=True),
        lax.all_gather(cotangent, "tp", axis=1, tiled=True),
    )
    packed, scaled = pack_rows(select, weighted, whole_tokens, whole_grads)
    rows_in, grads_in = (
        lax.all_to_all(packed, "ep", split_axis=0, concat_axis=0, tiled=True),
        lax.all_to_all(scaled, "ep", split_axis=0, concat_axis=0, tiled=True),
    )
    width = rows_in.shape[2]
    token_rows = rows_in.reshape(-1, width)
    grad_rows = grads_in.reshape(-1, width)
    gate_up = jnp.einsum(
        "rd,jfd->jrf", token_rows, expert_weights[:2], preferred_element_type=jnp.float32
    )
    gate_val = gate_up[0]
    up_val = gate_up[1]
    gate_weight = expert_weights[0]
    up_weight = expert_weights[1]
    down_weight = expert_weights[2]
    sigmoid_gate = jax.nn.sigmoid(gate_val)
    active = gate_val * sigmoid_gate
    hidden = (active * up_val).astype(jnp.bfloat16)
    out_part = jnp.dot(hidden, down_weight, preferred_element_type=jnp.float32)
    contract_last = (((1,), (1,)), ((), ()))
    d_hidden = lax.dot_general(
        grad_rows, down_weight, contract_last, preferred_element_type=jnp.float32
    )
    d_gate = (d_hidden * up_val * sigmoid_gate * (1.0 + gate_val * (1.0 - sigmoid_gate))).astype(
        jnp.bfloat16
    )
    d_up = (d_hidden * active).astype(jnp.bfloat16)
    back_part = jnp.dot(d_gate, gate_weight, preferred_element_type=jnp.float32) + jnp.dot(
        d_up, up_weight, preferred_element_type=jnp.float32
    )
    replicas = lax.axis_size("edp")
    rows_block, grads_block = (
        lax.all_to_all(token_rows, "edp", split_axis=1, concat_axis=0, tiled=True),
        lax.all_to_all(grad_rows, "edp", split_axis=1, concat_axis=0, tiled=True),
    )
    left_factors = lax.all_gather(jnp.stack([d_gate, d_up, hidden]), "edp", axis=1, tiled=True)
    block_width = rows_block.shape[1]
    rows_block = rows_block.reshape(replicas, -1, block_width)
    grads_block = grads_block.reshape(replicas, -1, block_width)
    left_factors = left_factors.reshape(3, replicas, -1, left_factors.shape[2])
    weight_grads = jnp.stack(
        [
            replica_sum(left_factors[0], rows_block),
            replica_sum(left_factors[1], rows_block),
            replica_sum(left_factors[2], grads_block),
        ]
    )
    out_sum, back_sum = (
        lax.psum_scatter(
            out_part.astype(jnp.bfloat16), "tp", scatter_dimension=1, tiled=True
        ).astype(jnp.float32),
        lax.psum_scatter(
            back_part.astype(jnp.bfloat16), "tp", scatter_dimension=1, tiled=True
        ).astype(jnp.float32),
    )
    home_out, home_back = (
        lax.all_to_all(
            out_sum.astype(jnp.bfloat16).reshape(n_devices, CAP, -1),
            "ep",
            split_axis=0,
            concat_axis=0,
            tiled=True,
        ),
        lax.all_to_all(
            back_sum.astype(jnp.bfloat16).reshape(n_devices, CAP, -1),
            "ep",
            split_axis=0,
            concat_axis=0,
            tiled=True,
        ),
    )
    pair_out = home_out.astype(jnp.float32).reshape(window, 4, CAP, -1).sum(axis=1)
    pair_back = home_back.astype(jnp.float32).reshape(window, 4, CAP, -1).sum(axis=1)
    mixed = jnp.einsum("tec,ecd->td", weighted, pair_out, precision=lax.Precision.HIGHEST).astype(
        jnp.bfloat16
    )
    grad_tokens = jnp.einsum(
        "tec,ecd->td", select, pair_back, precision=lax.Precision.HIGHEST
    ).astype(jnp.bfloat16)
    return (mixed, grad_tokens, weight_grads)


def solution(mesh):
    placed = (
        P(("ep", "edp"), "tp"),
        P(("ep", "edp"), "tp"),
        P(("ep", "edp"), None),
        P(("ep", "edp"), None),
        P(None, ("ep", "tp"), None),
    )
    return jax.shard_map(
        shards,
        mesh=mesh,
        in_specs=placed,
        out_specs=(P(("ep", "edp"), "tp"), P(("ep", "edp"), "tp"), P(None, ("ep", "tp"), "edp")),
        check_vma=False,
    )
```

profile of v0, /device:TPU:0, one launch (start us, length us, event | category | flops | bytes accessed | tf_op | source)
XLA Modules:
  0.0 122.3 jit_solution(8222102204199329675)
XLA Ops:
  11.3 10.0 %all-gather.3.cloned.1.call-done = bf16[128,4096]{1,0:T(8,128)(2,1)} async-done(((bf16[128,2048]{1,0:T(8,128)(2,1)}), bf16[128,4096]{1,0:T(8,128)(2,1)}) %all-gather.3.cloned.1.call-update) | async-done | bytes 1048592 | tf_op jit(solution)/shard_map/all_gather | solution.py:43
  23.6 3.9 %all-to-all-start = ((bf16[4,10,4096]{2,1,0:T(8,128)(2,1)}), bf16[4,10,4096]{2,1,0:T(8,128)(2,1)S(1)}, u32[]{:S(2)}, u32[]{:S(2)}) async-start(bf16[4,10,4096]{2,1,0:T(8,128)(2,1)} %reshape.215), calls=%async_computation | async-start | bytes 1048576 | tf_op jit(solution)/shard_map/all_to_all | solution.py:48
  27.6 5.5 %all-gather.5.cloned.1.call-done = bf16[128,4096]{1,0:T(8,128)(2,1)} async-done(((bf16[128,2048]{1,0:T(8,128)(2,1)}), bf16[128,4096]{1,0:T(8,128)(2,1)}) %all-gather.5.cloned.1.call-update) | async-done | bytes 1048592 | tf_op jit(solution)/shard_map/all_gather | solution.py:44
  33.1 1.7 %convolution_convert_fusion.1 = bf16[10,4096]{1,0:T(8,128)(2,1)S(1)} fusion(f32[128,10]{0,1:T(8,128)S(1)} %get-tuple-element.4, bf16[128,4096]{1,0:T(8,128)(2,1)} %all-gather.5.cloned.1.call-done), kind=kOutput, calls=%fused_computation.3 | convolution fusion | flops 62955520 | bytes 1135616 | tf_op jit(solution)/shard_map/tec,td->ecd/dot_general | solution.py:26
  36.9 3.5 %all-to-all-start.2 = ((bf16[4,10,4096]{2,1,0:T(8,128)(2,1)}), bf16[4,10,4096]{2,1,0:T(8,128)(2,1)S(1)}, u32[]{:S(2)}, u32[]{:S(2)}) async-start(bf16[4,10,4096]{2,1,0:T(8,128)(2,1)} %reshape.218), calls=%async_computation.3 | async-start | bytes 1048576 | tf_op jit(solution)/shard_map/all_to_all | solution.py:49
  40.5 3.0 %fusion.13 = f32[2,40,192]{2,1,0:T(8,128)S(1)} fusion(bf16[40,4096,1]{1,0,2:T(8,128)(2,1)S(1)} %reshape.222, bf16[3,192,4096]{2,1,0:T(8,128)(2,1)} %param.9), kind=kOutput, calls=%fused_computation.26 | convolution fusion | flops 125829120 | bytes 3534848 | tf_op jit(solution)/shard_map/rd,jfd->jrf/dot_general | solution.py:54
  43.5 4.6 %all-to-all-done.2 = bf16[4,10,4096]{2,1,0:T(8,128)(2,1)S(1)} async-done(((bf16[4,10,4096]{2,1,0:T(8,128)(2,1)}), bf16[4,10,4096]{2,1,0:T(8,128)(2,1)S(1)}, u32[]{:S(2)}, u32[]{:S(2)}) %all-to-all-start.2) | async-done | bytes 327712 | tf_op jit(solution)/shard_map/all_to_all | solution.py:49
  48.2 2.0 %fusion.27 = (bf16[40,192]{1,0:T(8,128)(2,1)S(1)}, bf16[40,192]{1,0:T(8,128)(2,1)S(1)}) fusion(f32[2,40,192]{2,1,0:T(8,128)S(1)} %fusion.13, bf16[40,4096]{1,0:T(8,128)(2,1)S(1)} %reshape.219, bf16[3,192,4096]{2,1,0:T(8,128)(2,1)} %param.9), kind=kOutput, calls=%fused_computation.46 | convolution fusion | flops 63014400 | bytes 1992704 | tf_op jit(solution)/shard_map/dot_general | solution.py:67
  50.2 1.8 %fusion.4 = f32[40,4096]{1,0:T(8,128)S(1)} fusion(bf16[40,192]{1,0:T(8,128)(2,1)S(1)} %get-tuple-element.11, bf16[3,192,4096]{2,1,0:T(8,128)(2,1)} %param.9), kind=kOutput, calls=%fused_computation.17 | convolution fusion | flops 62914560 | bytes 2243584 | tf_op jit(solution)/shard_map/dot_general | solution.py:74
  52.0 2.5 %fusion = bf16[40,4096]{1,0:T(8,128)(2,1)} fusion(f32[40,4096]{1,0:T(8,128)S(1)} %fusion.4, bf16[40,192]{1,0:T(8,128)(2,1)S(1)} %get-tuple-element.10, bf16[3,192,4096]{2,1,0:T(8,128)(2,1)} %param.9), kind=kOutput, calls=%fused_computation.1 | convolution fusion | flops 63242240 | bytes 2571264 | tf_op jit(solution)/shard_map/dot_general | solution.py:74
  55.6 4.7 %all-to-all-start.4 = ((bf16[40,4,1024]{2,0,1:T(8,128)(2,1)}), bf16[40,4,1024]{2,0,1:T(8,128)(2,1)S(1)}, u32[]{:S(2)}, u32[]{:S(2)}) async-start(bf16[40,4,1024]{2,0,1:T(8,128)(2,1)} %copy.30), calls=%async_computation.6 | async-start | bytes 655360 | tf_op jit(solution)/shard_map/all_to_all | solution.py:79
  60.3 2.5 %convolution_convert_fusion = bf16[40,4096]{1,0:T(8,128)(2,1)} fusion(bf16[3,192,4096]{2,1,0:T(8,128)(2,1)} %param.9, bf16[1,40,192]{2,1,0:T(8,128)(2,1)S(1)} %multiply_convert_fusion), kind=kOutput, calls=%fused_computation.2 | convolution fusion | flops 63078400 | bytes 1915904 | tf_op jit(solution)/shard_map/dot_general | solution.py:65
  64.0 14.8 %all_gather.11 = bf16[3,160,192]{2,1,0:T(8,128)(2,1)S(1)} all-gather(bf16[3,40,192]{2,1,0:T(8,128)(2,1)S(1)} %pad_maximum_fusion.1), channel_id=1, replica_groups=mesh['ep'=4,'edp'=4,'tp'=2] {'edp'}, dimensions={1}, use_global_device_ids=true | all-gather | bytes 230400 | tf_op jit(solution)/shard_map/all_gather | solution.py:82
  79.5 4.1 %all-to-all-start.5 = ((bf16[40,4,1024]{2,0,1:T(8,128)(2,1)}), bf16[40,4,1024]{2,0,1:T(8,128)(2,1)}, u32[]{:S(2)}, u32[]{:S(2)}) async-start(bf16[40,4,1024]{2,0,1:T(8,128)(2,1)} %copy.31), calls=%async_computation.7 | async-start | bytes 655360 | tf_op jit(solution)/shard_map/all_to_all | solution.py:80
  85.7 5.3 %all-to-all-done.5 = bf16[40,4,1024]{2,0,1:T(8,128)(2,1)} async-done(((bf16[40,4,1024]{2,0,1:T(8,128)(2,1)}), bf16[40,4,1024]{2,0,1:T(8,128)(2,1)}, u32[]{:S(2)}, u32[]{:S(2)}) %all-to-all-start.5) | async-done | bytes 327712 | tf_op jit(solution)/shard_map/all_to_all | solution.py:80
  91.0 1.6 %convolution_convert_fusion.5 = bf16[4,192,1024]{2,1,0:T(8,128)(2,1)S(1)} fusion(bf16[4,40,192]{2,1,0:T(8,128)(2,1)S(1)} %bitcast.86, bf16[40,4,1024]{2,0,1:T(8,128)(2,1)} %all-to-all-done.5), kind=kOutput, calls=%fused_computation.13 | convolution fusion | flops 63700992 | bytes 1961984 | tf_op jit(solution)/shard_map/prs,prd->psd/dot_general | solution.py:33
  94.3 1.7 %reshape.220 = bf16[4,10,2048]{2,1,0:T(8,128)(2,1)} reshape(bf16[40,2048]{1,0:T(8,128)(2,1)} %reduce-scatter.5.cloned.1.call-done) | data formatting | bytes 327680 | tf_op jit(solution)/shard_map/reshape | solution.py:111
  96.0 3.4 %all-to-all-start.3 = ((bf16[4,10,2048]{2,1,0:T(8,128)(2,1)}), bf16[4,10,2048]{2,1,0:T(8,128)(2,1)S(1)}, u32[]{:S(2)}, u32[]{:S(2)}) async-start(bf16[4,10,2048]{2,1,0:T(8,128)(2,1)} %reshape.220), calls=%async_computation.5 | async-start | bytes 524288 | tf_op jit(solution)/shard_map/all_to_all | solution.py:110
  101.0 1.7 %reshape.217 = bf16[4,10,2048]{2,1,0:T(8,128)(2,1)} reshape(bf16[40,2048]{1,0:T(8,128)(2,1)} %reduce-scatter.3.cloned.1.call-done) | data formatting | bytes 327680 | tf_op jit(solution)/shard_map/reshape | solution.py:104
  102.7 2.4 %all-to-all-done.3 = bf16[4,10,2048]{2,1,0:T(8,128)(2,1)S(1)} async-done(((bf16[4,10,2048]{2,1,0:T(8,128)(2,1)}), bf16[4,10,2048]{2,1,0:T(8,128)(2,1)S(1)}, u32[]{:S(2)}, u32[]{:S(2)}) %all-to-all-start.3) | async-done | bytes 163872 | tf_op jit(solution)/shard_map/all_to_all | solution.py:110
  105.1 3.4 %all-to-all-start.1 = ((bf16[4,10,2048]{2,1,0:T(8,128)(2,1)}), bf16[4,10,2048]{2,1,0:T(8,128)(2,1)S(1)}, u32[]{:S(2)}, u32[]{:S(2)}) async-start(bf16[4,10,2048]{2,1,0:T(8,128)(2,1)} %reshape.217), calls=%async_computation.2 | async-start | bytes 524288 | tf_op jit(solution)/shard_map/all_to_all | solution.py:103
  108.6 1.8 %convolution_convert_fusion.3 = bf16[128,2048]{1,0:T(8,128)(2,1)} fusion(f32[128,10]{0,1:T(8,128)S(1)} %copy-done.4, f32[10,2048]{1,0:T(8,128)S(1)} %convert_reduce_fusion.3), kind=kOutput, calls=%fused_computation.10 | convolution fusion | flops 31719424 | bytes 611328 | tf_op jit(solution)/shard_map/tec,ecd->td/dot_general | solution.py:123
  110.4 3.5 %all-to-all-done.1 = bf16[4,10,2048]{2,1,0:T(8,128)(2,1)S(1)} async-done(((bf16[4,10,2048]{2,1,0:T(8,128)(2,1)}), bf16[4,10,2048]{2,1,0:T(8,128)(2,1)S(1)}, u32[]{:S(2)}, u32[]{:S(2)}) %all-to-all-start.1) | async-done | bytes 163872 | tf_op jit(solution)/shard_map/all_to_all | solution.py:103
  113.9 1.8 %convolution_convert_fusion.4 = bf16[128,2048]{1,0:T(8,128)(2,1)} fusion(f32[128,10]{0,1:T(8,128)S(1)} %copy-done.2, f32[10,2048]{1,0:T(8,128)S(1)} %convert_reduce_fusion.4), kind=kOutput, calls=%fused_computation.11 | convolution fusion | flops 31719424 | bytes 611328 | tf_op jit(solution)/shard_map/tec,ecd->td/dot_general | solution.py:120
  (57 shorter events, 17.0 us)
Async XLA Ops:
  7.2 14.2 %all-gather.3.cloned.1.call-start = ((), (), s32[]{:S(2)}) async-start(), calls=%async_computation.8 | async-start | bytes 1572864 | tf_op jit(solution)/shard_map/all_gather | solution.py:43
  7.9 25.2 %all-gather.5.cloned.1.call-start = ((), (), s32[]{:S(2)}) async-start(), calls=%async_computation.10 | async-start | bytes 1572864 | tf_op jit(solution)/shard_map/all_gather | solution.py:44
  11.3 12.3 %copy-start.3 = (f32[128,10]{0,1:T(8,128)}, f32[128,10]{0,1:T(8,128)S(1)}, u32[]{:S(2)}) copy-start(f32[128,10]{0,1:T(8,128)S(1)} %get-tuple-element.3) | copy-start | bytes 15364
  11.3 25.5 %copy-start.1 = (f32[128,10]{0,1:T(8,128)}, f32[128,10]{0,1:T(8,128)S(1)}, u32[]{:S(2)}) copy-start(f32[128,10]{0,1:T(8,128)S(1)} %get-tuple-element.4) | copy-start | bytes 15364
  23.6 12.4 %all-to-all-start = ((bf16[4,10,4096]{2,1,0:T(8,128)(2,1)}), bf16[4,10,4096]{2,1,0:T(8,128)(2,1)S(1)}, u32[]{:S(2)}, u32[]{:S(2)}) async-start(bf16[4,10,4096]{2,1,0:T(8,128)(2,1)} %reshape.215), calls=%async_computation | async-start | bytes 1048576 | tf_op jit(solution)/shard_map/all_to_all | solution.py:48
  36.9 11.2 %all-to-all-start.2 = ((bf16[4,10,4096]{2,1,0:T(8,128)(2,1)}), bf16[4,10,4096]{2,1,0:T(8,128)(2,1)S(1)}, u32[]{:S(2)}, u32[]{:S(2)}) async-start(bf16[4,10,4096]{2,1,0:T(8,128)(2,1)} %reshape.218), calls=%async_computation.3 | async-start | bytes 1048576 | tf_op jit(solution)/shard_map/all_to_all | solution.py:49
  40.3 54.0 %reduce-scatter.5.cloned.1.call-start = ((), (), s32[]{:S(2)}) async-start(), calls=%async_computation.11 | async-start | bytes 491520 | tf_op jit(solution)/shard_map/reduce_scatter | solution.py:98
  55.6 23.8 %all-to-all-start.4 = ((bf16[40,4,1024]{2,0,1:T(8,128)(2,1)}), bf16[40,4,1024]{2,0,1:T(8,128)(2,1)S(1)}, u32[]{:S(2)}, u32[]{:S(2)}) async-start(bf16[40,4,1024]{2,0,1:T(8,128)(2,1)} %copy.30), calls=%async_computation.6 | async-start | bytes 655360 | tf_op jit(solution)/shard_map/all_to_all | solution.py:79
  60.3 40.7 %reduce-scatter.3.cloned.1.call-start = ((), (), s32[]{:S(2)}) async-start(), calls=%async_computation.9 | async-start | bytes 491520 | tf_op jit(solution)/shard_map/reduce_scatter | solution.py:95
  79.5 11.5 %all-to-all-start.5 = ((bf16[40,4,1024]{2,0,1:T(8,128)(2,1)}), bf16[40,4,1024]{2,0,1:T(8,128)(2,1)}, u32[]{:S(2)}, u32[]{:S(2)}) async-start(bf16[40,4,1024]{2,0,1:T(8,128)(2,1)} %copy.31), calls=%async_computation.7 | async-start | bytes 655360 | tf_op jit(solution)/shard_map/all_to_all | solution.py:80
  93.7 5.7 %copy-start = (f32[192,1024]{1,0:T(8,128)S(1)}, f32[192,1024]{1,0:T(8,128)}, u32[]{:S(2)}) copy-start(f32[192,1024]{1,0:T(8,128)} %convert_reduce_fusion.2) | copy-start | bytes 2359300
  96.0 9.1 %all-to-all-start.3 = ((bf16[4,10,2048]{2,1,0:T(8,128)(2,1)}), bf16[4,10,2048]{2,1,0:T(8,128)(2,1)S(1)}, u32[]{:S(2)}, u32[]{:S(2)}) async-start(bf16[4,10,2048]{2,1,0:T(8,128)(2,1)} %reshape.220), calls=%async_computation.5 | async-start | bytes 524288 | tf_op jit(solution)/shard_map/all_to_all | solution.py:110
  99.4 9.1 %copy-start.4 = (f32[128,10]{0,1:T(8,128)S(1)}, f32[128,10]{0,1:T(8,128)}, u32[]{:S(2)}) copy-start(f32[128,10]{0,1:T(8,128)} %copy-done.3) | copy-start | bytes 15364
  101.0 12.9 %copy-start.2 = (f32[128,10]{0,1:T(8,128)S(1)}, f32[128,10]{0,1:T(8,128)}, u32[]{:S(2)}) copy-start(f32[128,10]{0,1:T(8,128)} %copy-done.1) | copy-start | bytes 15364
  105.1 8.8 %all-to-all-start.1 = ((bf16[4,10,2048]{2,1,0:T(8,128)(2,1)}), bf16[4,10,2048]{2,1,0:T(8,128)(2,1)S(1)}, u32[]{:S(2)}, u32[]{:S(2)}) async-start(bf16[4,10,2048]{2,1,0:T(8,128)(2,1)} %reshape.217), calls=%async_computation.2 | async-start | bytes 524288 | tf_op jit(solution)/shard_map/all_to_all | solution.py:103
Sparse Core Ops, SparseCore 0:
  9.5 11.7 all-gather.2
  22.9 10.1 all-gather.4
  54.7 7.8 reduce-scatter.4
  65.3 8.8 reduce-scatter.2
where the time goes:
time: 123 us; the launch traced here: 122 us
  waiting for transfers between devices  33.9 us (28%)
  starting transfers between devices  23.1 us (19%)
  matrix products  22.4 us (18%)
  blocking collectives  14.8 us (12%)
  between operations  14 us (11%)
  local copies, waits for them, and re-layouts  8.74 us (7%)
  other arithmetic  5.3 us (4%)
    all_gather x1, blocking collectives, shards(): lax.all_gather(jnp.stack([d_gate, d_up, hidden]), 'edp', axis=1, tiled=True)  14.8 us
    all_gather x1, waiting for transfers between devices, shards(): lax.all_gather(tokens, 'tp', axis=1, tiled=True)  10 us
    all_gather x1, waiting for transfers between devices, shards(): lax.all_gather(cotangent, 'tp', axis=1, tiled=True)  5.55 us
    all_to_all x1, waiting for transfers between devices, shards(): lax.all_to_all(grad_rows, 'edp', split_axis=1, concat_axis=0, tiled=True)  5.29 us
    all_to_all x1, starting transfers between devices, shards(): lax.all_to_all(token_rows, 'edp', split_axis=1, concat_axis=0, tiled=True)  4.67 us
    all_to_all x1, waiting for transfers between devices, shards(): lax.all_to_all(scaled, 'ep', split_axis=0, concat_axis=0, tiled=True)  4.58 us
    all_to_all x1, starting transfers between devices, shards(): lax.all_to_all(grad_rows, 'edp', split_axis=1, concat_axis=0, tiled=True)  4.11 us
    all_to_all x1, starting transfers between devices, shards(): lax.all_to_all(packed, 'ep', split_axis=0, concat_axis=0, tiled=True)  3.92 us
  transfers between devices with their start and end apart: 10, of which 7 were waited for; matrix products, arithmetic and copies ran while one was open for 22% of the time, Pallas kernels for 0%

commit v1 on v0

--- a/solution.py
+++ b/solution.py
@@ -79,7 +79,16 @@
         lax.all_to_all(token_rows, "edp", split_axis=1, concat_axis=0, tiled=True),
         lax.all_to_all(grad_rows, "edp", split_axis=1, concat_axis=0, tiled=True),
     )
-    left_factors = lax.all_gather(jnp.stack([d_gate, d_up, hidden]), "edp", axis=1, tiled=True)
+    body = jnp.stack([d_gate, d_up, hidden])
+    left_factors = jnp.concatenate(
+        lax.all_to_all(
+            jnp.stack([body for _ in range(lax.axis_size("edp"))], axis=0),
+            axis_name="edp",
+            split_axis=0,
+            concat_axis=0,
+        ),
+        axis=1,
+    )
     block_width = rows_block.shape[1]
     rows_block = rows_block.reshape(replicas, -1, block_width)
     grads_block = grads_block.reshape(replicas, -1, block_width)

time: 123 us -> 118 us (0.959)
  blocking collectives: 14.8 us -> 0 us
  waiting for transfers between devices: 33.9 us -> 40.3 us
  starting transfers between devices: 23.1 us -> 26.5 us
    all_gather x1 -> x0, blocking collectives: 14.8 us -> none  [shards(): lax.all_gather(jnp.stack([d_gate, d_up, hidden]), 'edp', axis=1, tiled=True)]
    all_to_all x0 -> x1, starting transfers between devices: none -> 4.67 us  [shards(): lax.all_to_all(jnp.stack([body for _ in range(lax.axis_size('edp'))], axi...]
    all_to_all x1, waiting for transfers between devices: 0.01 us -> 3.56 us  [shards(): lax.all_to_all(token_rows, 'edp', split_axis=1, concat_axis=0, tiled=True)]
    all_to_all x0 -> x1, waiting for transfers between devices: none -> 3.19 us  [shards(): lax.all_to_all(jnp.stack([body for _ in range(lax.axis_size('edp'))], axi...]
  transfers between devices with their start and end apart: 10 -> 11, of which waited for: 7 -> 9; matrix products, arithmetic and copies ran while one was open for 22% -> 25% of each run, Pallas kernels for 0% -> 0%
where the time goes in v1:
time: 118 us; the launch traced here: 117 us
  waiting for transfers between devices  40.3 us (34%)
  starting transfers between devices  26.5 us (22%)
  matrix products  22.5 us (19%)
  between operations  14 us (12%)
  local copies, waits for them, and re-layouts  8.8 us (7%)
  other arithmetic  5.3 us (4%)
    all_gather x1, waiting for transfers between devices, shards(): lax.all_gather(tokens, 'tp', axis=1, tiled=True)  10 us
    all_gather x1, waiting for transfers between devices, shards(): lax.all_gather(cotangent, 'tp', axis=1, tiled=True)  5.55 us
    all_to_all x1, waiting for transfers between devices, shards(): lax.all_to_all(grad_rows, 'edp', split_axis=1, concat_axis=0, tiled=True)  5.21 us
    all_to_all x1, starting transfers between devices, shards(): lax.all_to_all(jnp.stack([body for _ in range(lax.axis_size('edp'))], axi...  4.67 us
    all_to_all x1, waiting for transfers between devices, shards(): lax.all_to_all(scaled, 'ep', split_axis=0, concat_axis=0, tiled=True)  4.6 us
    all_to_all x1, starting transfers between devices, shards(): lax.all_to_all(grad_rows, 'edp', split_axis=1, concat_axis=0, tiled=True)  4.09 us
    all_to_all x1, starting transfers between devices, shards(): lax.all_to_all(packed, 'ep', split_axis=0, concat_axis=0, tiled=True)  3.92 us
    dot_general x3, matrix products, replica_sum(): jnp.einsum('prs,prd->psd', left, right, preferred_element_type=jnp.float32)  3.76 us
  transfers between devices with their start and end apart: 11, of which 9 were waited for; matrix products, arithmetic and copies ran while one was open for 25% of the time, Pallas kernels for 0%

profile of v1, /device:TPU:0, one launch (start us, length us, event | category | flops | bytes accessed | tf_op | source)
XLA Modules:
  0.0 117.4 jit_solution(13325426099358148866)
XLA Ops:
  11.3 10.0 %all-gather.3.cloned.1.call-done = bf16[128,4096]{1,0:T(8,128)(2,1)} async-done(((bf16[128,2048]{1,0:T(8,128)(2,1)}), bf16[128,4096]{1,0:T(8,128)(2,1)}) %all-gather.3.cloned.1.call-update) | async-done | bytes 1048592 | tf_op jit(solution)/shard_map/all_gather | solution.py:43
  23.6 3.9 %all-to-all-start = ((bf16[4,10,4096]{2,1,0:T(8,128)(2,1)}), bf16[4,10,4096]{2,1,0:T(8,128)(2,1)S(1)}, u32[]{:S(2)}, u32[]{:S(2)}) async-start(bf16[4,10,4096]{2,1,0:T(8,128)(2,1)} %reshape.213), calls=%async_computation | async-start | bytes 1048576 | tf_op jit(solution)/shard_map/all_to_all | solution.py:48
  27.6 5.6 %all-gather.5.cloned.1.call-done = bf16[128,4096]{1,0:T(8,128)(2,1)} async-done(((bf16[128,2048]{1,0:T(8,128)(2,1)}), bf16[128,4096]{1,0:T(8,128)(2,1)}) %all-gather.5.cloned.1.call-update) | async-done | bytes 1048592 | tf_op jit(solution)/shard_map/all_gather | solution.py:44
  33.1 1.7 %convolution_convert_fusion.1 = bf16[10,4096]{1,0:T(8,128)(2,1)S(1)} fusion(f32[128,10]{0,1:T(8,128)S(1)} %get-tuple-element.4, bf16[128,4096]{1,0:T(8,128)(2,1)} %all-gather.5.cloned.1.call-done), kind=kOutput, calls=%fused_computation.3 | convolution fusion | flops 62955520 | bytes 1135616 | tf_op jit(solution)/shard_map/tec,td->ecd/dot_general | solution.py:26
  36.9 3.5 %all-to-all-start.2 = ((bf16[4,10,4096]{2,1,0:T(8,128)(2,1)}), bf16[4,10,4096]{2,1,0:T(8,128)(2,1)S(1)}, u32[]{:S(2)}, u32[]{:S(2)}) async-start(bf16[4,10,4096]{2,1,0:T(8,128)(2,1)} %reshape.216), calls=%async_computation.3 | async-start | bytes 1048576 | tf_op jit(solution)/shard_map/all_to_all | solution.py:49
  40.5 3.0 %fusion.13 = f32[2,40,192]{2,1,0:T(8,128)S(1)} fusion(bf16[40,4096,1]{1,0,2:T(8,128)(2,1)S(1)} %reshape.221, bf16[3,192,4096]{2,1,0:T(8,128)(2,1)} %param.9), kind=kOutput, calls=%fused_computation.26 | convolution fusion | flops 125829120 | bytes 3534848 | tf_op jit(solution)/shard_map/rd,jfd->jrf/dot_general | solution.py:54
  43.5 4.6 %all-to-all-done.2 = bf16[4,10,4096]{2,1,0:T(8,128)(2,1)S(1)} async-done(((bf16[4,10,4096]{2,1,0:T(8,128)(2,1)}), bf16[4,10,4096]{2,1,0:T(8,128)(2,1)S(1)}, u32[]{:S(2)}, u32[]{:S(2)}) %all-to-all-start.2) | async-done | bytes 327712 | tf_op jit(solution)/shard_map/all_to_all | solution.py:49
  48.2 2.0 %fusion.27 = (bf16[40,192]{1,0:T(8,128)(2,1)S(1)}, bf16[40,192]{1,0:T(8,128)(2,1)S(1)}) fusion(f32[2,40,192]{2,1,0:T(8,128)S(1)} %fusion.13, bf16[40,4096]{1,0:T(8,128)(2,1)S(1)} %reshape.217, bf16[3,192,4096]{2,1,0:T(8,128)(2,1)} %param.9), kind=kOutput, calls=%fused_computation.50 | convolution fusion | flops 63014400 | bytes 1992704 | tf_op jit(solution)/shard_map/dot_general | solution.py:67
  50.2 1.8 %fusion.4 = f32[40,4096]{1,0:T(8,128)S(1)} fusion(bf16[40,192]{1,0:T(8,128)(2,1)S(1)} %get-tuple-element.8, bf16[3,192,4096]{2,1,0:T(8,128)(2,1)} %param.9), kind=kOutput, calls=%fused_computation.17 | convolution fusion | flops 62914560 | bytes 2243584 | tf_op jit(solution)/shard_map/dot_general | solution.py:74
  52.8 4.7 %all-to-all-start.4 = ((bf16[4,3,40,192]{3,2,1,0:T(8,128)(2,1)}), bf16[4,3,40,192]{3,2,1,0:T(8,128)(2,1)S(1)}, u32[]{:S(2)}, u32[]{:S(2)}) async-start(bf16[4,3,40,192]{3,2,1,0:T(8,128)(2,1)} %stack.32), calls=%async_computation.6 | async-start | bytes 491520 | tf_op jit(solution)/shard_map/all_to_all | solution.py:84
  57.4 2.5 %fusion = bf16[40,4096]{1,0:T(8,128)(2,1)} fusion(f32[40,4096]{1,0:T(8,128)S(1)} %fusion.4, bf16[40,192]{1,0:T(8,128)(2,1)S(1)} %get-tuple-element.7, bf16[3,192,4096]{2,1,0:T(8,128)(2,1)} %param.9), kind=kOutput, calls=%fused_computation.1 | convolution fusion | flops 63242240 | bytes 2571264 | tf_op jit(solution)/shard_map/dot_general | solution.py:74
  61.0 3.2 %all-to-all-done.4 = bf16[4,3,40,192]{3,2,1,0:T(8,128)(2,1)S(1)} async-done(((bf16[4,3,40,192]{3,2,1,0:T(8,128)(2,1)}), bf16[4,3,40,192]{3,2,1,0:T(8,128)(2,1)S(1)}, u32[]{:S(2)}, u32[]{:S(2)}) %all-to-all-start.4) | async-done | bytes 184352 | tf_op jit(solution)/shard_map/all_to_all | solution.py:84
  64.2 3.5 %all-to-all-start.5 = ((bf16[40,4,1024]{2,0,1:T(8,128)(2,1)}), bf16[40,4,1024]{2,0,1:T(8,128)(2,1)S(1)}, u32[]{:S(2)}, u32[]{:S(2)}) async-start(bf16[40,4,1024]{2,0,1:T(8,128)(2,1)} %copy.41), calls=%async_computation.7 | async-start | bytes 655360 | tf_op jit(solution)/shard_map/all_to_all | solution.py:79
  68.8 2.5 %convolution_convert_fusion = bf16[40,4096]{1,0:T(8,128)(2,1)} fusion(bf16[3,192,4096]{2,1,0:T(8,128)(2,1)} %param.9, bf16[1,40,192]{2,1,0:T(8,128)(2,1)S(1)} %multiply_convert_fusion), kind=kOutput, calls=%fused_computation.2 | convolution fusion | flops 63078400 | bytes 1915904 | tf_op jit(solution)/shard_map/dot_general | solution.py:65
  71.4 3.6 %all-to-all-done.5 = bf16[40,4,1024]{2,0,1:T(8,128)(2,1)S(1)} async-done(((bf16[40,4,1024]{2,0,1:T(8,128)(2,1)}), bf16[40,4,1024]{2,0,1:T(8,128)(2,1)S(1)}, u32[]{:S(2)}, u32[]{:S(2)}) %all-to-all-start.5) | async-done | bytes 327712 | tf_op jit(solution)/shard_map/all_to_all | solution.py:79
  74.9 4.1 %all-to-all-start.6 = ((bf16[40,4,1024]{2,0,1:T(8,128)(2,1)}), bf16[40,4,1024]{2,0,1:T(8,128)(2,1)}, u32[]{:S(2)}, u32[]{:S(2)}) async-start(bf16[40,4,1024]{2,0,1:T(8,128)(2,1)} %copy.42), calls=%async_computation.8 | async-start | bytes 655360 | tf_op jit(solution)/shard_map/all_to_all | solution.py:80
  81.2 5.2 %all-to-all-done.6 = bf16[40,4,1024]{2,0,1:T(8,128)(2,1)} async-done(((bf16[40,4,1024]{2,0,1:T(8,128)(2,1)}), bf16[40,4,1024]{2,0,1:T(8,128)(2,1)}, u32[]{:S(2)}, u32[]{:S(2)}) %all-to-all-start.6) | async-done | bytes 327712 | tf_op jit(solution)/shard_map/all_to_all | solution.py:80
  91.5 3.4 %all-to-all-start.3 = ((bf16[4,10,2048]{2,1,0:T(8,128)(2,1)}), bf16[4,10,2048]{2,1,0:T(8,128)(2,1)S(1)}, u32[]{:S(2)}, u32[]{:S(2)}) async-start(bf16[4,10,2048]{2,1,0:T(8,128)(2,1)} %reshape.218), calls=%async_computation.5 | async-start | bytes 524288 | tf_op jit(solution)/shard_map/all_to_all | solution.py:119
  96.5 1.7 %reshape.215 = bf16[4,10,2048]{2,1,0:T(8,128)(2,1)} reshape(bf16[40,2048]{1,0:T(8,128)(2,1)} %reduce-scatter.3.cloned.1.call-done) | data formatting | bytes 327680 | tf_op jit(solution)/shard_map/reshape | solution.py:113
  98.1 2.1 %all-to-all-done.3 = bf16[4,10,2048]{2,1,0:T(8,128)(2,1)S(1)} async-done(((bf16[4,10,2048]{2,1,0:T(8,128)(2,1)}), bf16[4,10,2048]{2,1,0:T(8,128)(2,1)S(1)}, u32[]{:S(2)}, u32[]{:S(2)}) %all-to-all-start.3) | async-done | bytes 163872 | tf_op jit(solution)/shard_map/all_to_all | solution.py:119
  100.3 3.4 %all-to-all-start.1 = ((bf16[4,10,2048]{2,1,0:T(8,128)(2,1)}), bf16[4,10,2048]{2,1,0:T(8,128)(2,1)S(1)}, u32[]{:S(2)}, u32[]{:S(2)}) async-start(bf16[4,10,2048]{2,1,0:T(8,128)(2,1)} %reshape.215), calls=%async_computation.2 | async-start | bytes 524288 | tf_op jit(solution)/shard_map/all_to_all | solution.py:112
  103.7 1.8 %convolution_convert_fusion.3 = bf16[128,2048]{1,0:T(8,128)(2,1)} fusion(f32[128,10]{0,1:T(8,128)S(1)} %get-tuple-element.3, f32[10,2048]{1,0:T(8,128)S(1)} %convert_reduce_fusion.3), kind=kOutput, calls=%fused_computation.10 | convolution fusion | flops 31719424 | bytes 611328 | tf_op jit(solution)/shard_map/tec,ecd->td/dot_general | solution.py:132
  105.6 3.5 %all-to-all-done.1 = bf16[4,10,2048]{2,1,0:T(8,128)(2,1)S(1)} async-done(((bf16[4,10,2048]{2,1,0:T(8,128)(2,1)}), bf16[4,10,2048]{2,1,0:T(8,128)(2,1)S(1)}, u32[]{:S(2)}, u32[]{:S(2)}) %all-to-all-start.1) | async-done | bytes 163872 | tf_op jit(solution)/shard_map/all_to_all | solution.py:112
  109.1 1.8 %convolution_convert_fusion.4 = bf16[128,2048]{1,0:T(8,128)(2,1)} fusion(f32[128,10]{0,1:T(8,128)S(1)} %get-tuple-element.4, f32[10,2048]{1,0:T(8,128)S(1)} %convert_reduce_fusion.4), kind=kOutput, calls=%fused_computation.11 | convolution fusion | flops 31719424 | bytes 611328 | tf_op jit(solution)/shard_map/tec,ecd->td/dot_general | solution.py:129
  (53 shorter events, 20.4 us)
Async XLA Ops:
  7.2 14.2 %all-gather.3.cloned.1.call-start = ((), (), s32[]{:S(2)}) async-start(), calls=%async_computation.9 | async-start | bytes 1572864 | tf_op jit(solution)/shard_map/all_gather | solution.py:43
  7.9 25.2 %all-gather.5.cloned.1.call-start = ((), (), s32[]{:S(2)}) async-start(), calls=%async_computation.11 | async-start | bytes 1572864 | tf_op jit(solution)/shard_map/all_gather | solution.py:44
  23.6 12.4 %all-to-all-start = ((bf16[4,10,4096]{2,1,0:T(8,128)(2,1)}), bf16[4,10,4096]{2,1,0:T(8,128)(2,1)S(1)}, u32[]{:S(2)}, u32[]{:S(2)}) async-start(bf16[4,10,4096]{2,1,0:T(8,128)(2,1)} %reshape.213), calls=%async_computation | async-start | bytes 1048576 | tf_op jit(solution)/shard_map/all_to_all | solution.py:48
  36.9 11.2 %all-to-all-start.2 = ((bf16[4,10,4096]{2,1,0:T(8,128)(2,1)}), bf16[4,10,4096]{2,1,0:T(8,128)(2,1)S(1)}, u32[]{:S(2)}, u32[]{:S(2)}) async-start(bf16[4,10,4096]{2,1,0:T(8,128)(2,1)} %reshape.216), calls=%async_computation.3 | async-start | bytes 1048576 | tf_op jit(solution)/shard_map/all_to_all | solution.py:49
  52.8 11.5 %all-to-all-start.4 = ((bf16[4,3,40,192]{3,2,1,0:T(8,128)(2,1)}), bf16[4,3,40,192]{3,2,1,0:T(8,128)(2,1)S(1)}, u32[]{:S(2)}, u32[]{:S(2)}) async-start(bf16[4,3,40,192]{3,2,1,0:T(8,128)(2,1)} %stack.32), calls=%async_computation.6 | async-start | bytes 491520 | tf_op jit(solution)/shard_map/all_to_all | solution.py:84
  57.4 32.4 %reduce-scatter.5.cloned.1.call-start = ((), (), s32[]{:S(2)}) async-start(), calls=%async_computation.12 | async-start | bytes 491520 | tf_op jit(solution)/shard_map/reduce_scatter | solution.py:107
  64.2 10.7 %all-to-all-start.5 = ((bf16[40,4,1024]{2,0,1:T(8,128)(2,1)}), bf16[40,4,1024]{2,0,1:T(8,128)(2,1)S(1)}, u32[]{:S(2)}, u32[]{:S(2)}) async-start(bf16[40,4,1024]{2,0,1:T(8,128)(2,1)} %copy.41), calls=%async_computation.7 | async-start | bytes 655360 | tf_op jit(solution)/shard_map/all_to_all | solution.py:79
  67.7 28.8 %reduce-scatter.3.cloned.1.call-start = ((), (), s32[]{:S(2)}) async-start(), calls=%async_computation.10 | async-start | bytes 491520 | tf_op jit(solution)/shard_map/reduce_scatter | solution.py:104
  71.4 7.7 %copy-start.1 = (bf16[4,3,40,192]{3,2,0,1:T(8,128)(2,1)}, bf16[4,3,40,192]{3,2,0,1:T(8,128)(2,1)S(1)}, u32[]{:S(2)}) copy-start(bf16[4,3,40,192]{3,2,0,1:T(8,128)(2,1)S(1)} %copy.44) | copy-start | bytes 552964
  74.9 11.5 %all-to-all-start.6 = ((bf16[40,4,1024]{2,0,1:T(8,128)(2,1)}), bf16[40,4,1024]{2,0,1:T(8,128)(2,1)}, u32[]{:S(2)}, u32[]{:S(2)}) async-start(bf16[40,4,1024]{2,0,1:T(8,128)(2,1)} %copy.42), calls=%async_computation.8 | async-start | bytes 655360 | tf_op jit(solution)/shard_map/all_to_all | solution.py:80
  89.2 5.7 %copy-start = (f32[192,1024]{1,0:T(8,128)S(1)}, f32[192,1024]{1,0:T(8,128)}, u32[]{:S(2)}) copy-start(f32[192,1024]{1,0:T(8,128)} %convert_reduce_fusion.2) | copy-start | bytes 2359300
  91.5 8.8 %all-to-all-start.3 = ((bf16[4,10,2048]{2,1,0:T(8,128)(2,1)}), bf16[4,10,2048]{2,1,0:T(8,128)(2,1)S(1)}, u32[]{:S(2)}, u32[]{:S(2)}) async-start(bf16[4,10,2048]{2,1,0:T(8,128)(2,1)} %reshape.218), calls=%async_computation.5 | async-start | bytes 524288 | tf_op jit(solution)/shard_map/all_to_all | solution.py:119
  100.3 8.8 %all-to-all-start.1 = ((bf16[4,10,2048]{2,1,0:T(8,128)(2,1)}), bf16[4,10,2048]{2,1,0:T(8,128)(2,1)S(1)}, u32[]{:S(2)}, u32[]{:S(2)}) async-start(bf16[4,10,2048]{2,1,0:T(8,128)(2,1)} %reshape.215), calls=%async_computation.2 | async-start | bytes 524288 | tf_op jit(solution)/shard_map/all_to_all | solution.py:112
Sparse Core Ops, SparseCore 0:
  9.5 11.7 all-gather.2
  22.9 10.1 all-gather.4
  61.0 8.2 reduce-scatter.4
  72.0 8.8 reduce-scatter.2
